TPU v7x, 32 devices: a whole 2x2x4 slice. The times are simulated.
32 devices in a mesh: grp: 8 (over z, y), mem: 4 (over x, core).
Axes of the slice: x: 2, y: 2, z: 4, core: 2. Of those that a mesh axis runs over, the one named last changes fastest.
Arguments:
- queries: bfloat16 [8192, 2048], P(('grp', 'mem')), may hold values from -6 to 6
- keys: bfloat16 [8192, 2048], P(('grp', 'mem')), may hold values from -6 to 6
- values: bfloat16 [8192, 2048], P(('grp', 'mem')), may hold values from -6 to 6
- grad_out: bfloat16 [8192, 2048], P(('grp', 'mem')), may hold values from -0.125 to 0.125
- log_decay: float32 [8, 8192], P(None, ('grp', 'mem')), may hold values from -1.6 to 0
Outputs:
- grad_queries: bfloat16 [8192, 2048], P(('grp', 'mem'))
- grad_keys: bfloat16 [8192, 2048], P(('grp', 'mem'))
- grad_values: bfloat16 [8192, 2048], P(('grp', 'mem'))
All inputs are finite; a program needn't handle non-finite values.
Results may differ from a plain program's by a relative error of at most 0.0052.
Values sent between devices are 32-bit elements; how exact they have to be, the bound alone decides.
A program may use at most 128 MiB of HBM per device.

v0:
```python
import jax
import jax.numpy as jnp
from jax import lax
from jax.sharding import PartitionSpec as P

HEAD_COUNT = 8
DK = 256
DV = 256
BLOCK = 128


def prefix(value, axis, join, neutral, backward):
    count, mine = (lax.axis_size(axis), lax.axis_index(axis))
    pieces = jax.tree.map(lambda part: lax.all_gather(part, axis), value)
    if backward:
        pieces = jax.tree.map(lambda part: part[::-1], pieces)
        mine = count - 1 - mine
    total = jax.tree.map(
        lambda part, zero: jnp.full_like(part, 0) + jnp.asarray(zero, part.dtype), value, neutral
    )

    def turn(position, total):
        longer = join(total, jax.tree.map(lambda part: part[position], pieces))
        return jax.tree.map(lambda new, old: jnp.where(position < mine, new, old), longer, total)

    return lax.fori_loop(0, count - 1, turn, total)


def chain(earlier, later):
    early_decay, early_state = earlier
    late_decay, late_state = later
    return (early_decay * late_decay, late_state + late_decay[:, None, None] * early_state)


def body(queries, keys, values, grad_out, log_decay):
    tokens = queries.shape[0]
    count = tokens // BLOCK
    scale = DK ** (-0.5)
    query_blocks = queries.reshape(count, BLOCK, HEAD_COUNT, DK)
    key_blocks = keys.reshape(count, BLOCK, HEAD_COUNT, DK)
    value_blocks = values.reshape(count, BLOCK, HEAD_COUNT, DV)
    grad_blocks = grad_out.reshape(count, BLOCK, HEAD_COUNT, DV)
    logs = jnp.transpose(log_decay.reshape(HEAD_COUNT, count, BLOCK), (1, 0, 2))
    cumul = jnp.cumsum(logs, axis=2)
    ends = cumul[:, :, -1]
    lower = jnp.tril(jnp.ones((BLOCK, BLOCK), dtype=bool))
    spread = cumul[:, :, :, None] - cumul[:, :, None, :]
    decay = jnp.where(lower, jnp.exp(jnp.where(lower, spread, 0.0)), 0.0)
    scores = jnp.einsum(
        "bthe,bshe->bhts", grad_blocks, value_blocks, preferred_element_type=jnp.float32
    )
    weight_grad = (scores * decay).astype(jnp.bfloat16)
    attend = jnp.einsum(
        "bthd,bshd->bhts", query_blocks, key_blocks, preferred_element_type=jnp.float32
    )
    weight_value = (attend * decay).astype(jnp.bfloat16)
    inner_query = jnp.einsum(
        "bhts,bshd->bthd", weight_grad, key_blocks, preferred_element_type=jnp.float32
    )
    inner_key = jnp.einsum(
        "bhts,bthd->bshd", weight_grad, query_blocks, preferred_element_type=jnp.float32
    )
    inner_value = jnp.einsum(
        "bhts,bthe->bshe", weight_value, grad_blocks, preferred_element_type=jnp.float32
    )
    head_factor = jnp.exp(jnp.transpose(cumul, (0, 2, 1)))[..., None]
    tail_factor = jnp.exp(jnp.transpose(ends[:, :, None] - cumul, (0, 2, 1)))[..., None]
    keys_decayed = (key_blocks * tail_factor).astype(jnp.bfloat16)
    queries_decayed = (query_blocks * head_factor).astype(jnp.bfloat16)
    forward_parts = jnp.einsum(
        "bshd,bshe->bhde", keys_decayed, value_blocks, preferred_element_type=jnp.float32
    )
    reverse_parts = jnp.einsum(
        "bthd,bthe->bhde", queries_decayed, grad_blocks, preferred_element_type=jnp.float32
    )
    block_decay = jnp.exp(ends)
    running = jnp.zeros((HEAD_COUNT, DK, DV), jnp.float32)
    carried = jnp.ones((HEAD_COUNT,), jnp.float32)
    prefix_list = []
    carried_list = []
    for position in range(count):
        prefix_list.append(running)
        carried_list.append(carried)
        running = block_decay[position][:, None, None] * running + forward_parts[position]
        carried = carried * block_decay[position]
    forward_total = running
    running = jnp.zeros((HEAD_COUNT, DK, DV), jnp.float32)
    after = jnp.ones((HEAD_COUNT,), jnp.float32)
    suffix_list = [None] * count
    after_list = [None] * count
    for position in reversed(range(count)):
        suffix_list[position] = running
        after_list[position] = after
        running = block_decay[position][:, None, None] * running + reverse_parts[position]
        after = after * block_decay[position]
    members = lax.axis_size("mem")
    decay_cols = jnp.broadcast_to(carried[None, :, None, None], (1, HEAD_COUNT, members, 1))
    pieces = (
        lax.all_to_all(decay_cols, "mem", split_axis=2, concat_axis=0, tiled=True),
        lax.all_to_all(forward_total[None], "mem", split_axis=2, concat_axis=0, tiled=True),
        lax.all_to_all(running[None], "mem", split_axis=2, concat_axis=0, tiled=True),
    )
    member_decays = pieces[0][:, :, 0, 0]
    width = DK // members
    share_identity = (
        jnp.ones((HEAD_COUNT,), jnp.float32),
        jnp.zeros((HEAD_COUNT, width, DV), jnp.float32),
    )
    forward_prefix = []
    accum = share_identity
    for index in range(members):
        forward_prefix.append(accum)
        accum = chain(accum, (member_decays[index], pieces[1][index]))
    forward_whole = accum
    reverse_prefix = [None] * members
    accum = share_identity
    for index in reversed(range(members)):
        reverse_prefix[index] = accum
        accum = chain(accum, (member_decays[index], pieces[2][index]))
    group_first = prefix(forward_whole, "grp", chain, share_identity, False)
    group_second = prefix(accum, "grp", chain, share_identity, True)
    first_stack = jnp.stack(
        [chain(group_first, forward_prefix[index])[1] for index in range(members)]
    )
    second_stack = jnp.stack(
        [chain(group_second, reverse_prefix[index])[1] for index in range(members)]
    )
    returned = (
        lax.all_to_all(first_stack, "mem", split_axis=0, concat_axis=2, tiled=True),
        lax.all_to_all(second_stack, "mem", split_axis=0, concat_axis=2, tiled=True),
    )
    state_from = returned[0][0]
    grads_from = returned[1][0]
    states_low = (
        jnp.stack(prefix_list) + jnp.stack(carried_list)[:, :, None, None] * state_from[None]
    ).astype(jnp.bfloat16)
    grads_low = (
        jnp.stack(suffix_list) + jnp.stack(after_list)[:, :, None, None] * grads_from[None]
    ).astype(jnp.bfloat16)
    outer_query = jnp.einsum(
        "bthe,bhde->bthd", grad_blocks, states_low, preferred_element_type=jnp.float32
    )
    outer_key = jnp.einsum(
        "bshe,bhde->bshd", value_blocks, grads_low, preferred_element_type=jnp.float32
    )
    outer_value = jnp.einsum(
        "bshd,bhde->bshe", key_blocks, grads_low, preferred_element_type=jnp.float32
    )
    grad_queries = (scale * (inner_query + head_factor * outer_query)).astype(jnp.bfloat16)
    grad_keys = (scale * (inner_key + tail_factor * outer_key)).astype(jnp.bfloat16)
    grad_values = (scale * (inner_value + tail_factor * outer_value)).astype(jnp.bfloat16)
    return (
        grad_queries.reshape(tokens, HEAD_COUNT * DK),
        grad_keys.reshape(tokens, HEAD_COUNT * DK),
        grad_values.reshape(tokens, HEAD_COUNT * DV),
    )


def solution(mesh):
    placed = (
        P(("grp", "mem"), None),
        P(("grp", "mem"), None),
        P(("grp", "mem"), None),
        P(("grp", "mem"), None),
        P(None, ("grp", "mem")),
    )
    return jax.shard_map(
        body,
        mesh=mesh,
        in_specs=placed,
        out_specs=(P(("grp", "mem"), None), P(("grp", "mem"), None), P(("grp", "mem"), None)),
        check_vma=False,
    )
```

profile of v0, /device:TPU:0, one launch (start us, length us, event | category | flops | bytes accessed | tf_op | source)
XLA Modules:
  0.0 301.0 jit_solution(9682326019785282810)
XLA Ops:
  9.3 4.2 %all-to-all-start.1 = ((f32[1,8,4,1]{1,3,0,2:T(1,128)}), f32[1,8,4,1]{1,3,0,2:T(1,128)S(1)}, u32[]{:S(2)}, u32[]{:S(2)}) async-start(f32[1,8,4,1]{1,3,0,2:T(1,128)} %broadcast_in_dim.21), calls=%async_computation.1 | async-start | bytes 4096 | tf_op jit(solution)/shard_map/all_to_all | solution.py:99
  20.3 2.9 slice_add_fusion
  23.2 2.6 copy.103
  25.8 4.5 %all-to-all-start.3 = ((f32[1,8,256,256]{3,1,0,2:T(8,128)}), f32[1,8,256,256]{3,1,0,2:T(8,128)}, u32[]{:S(2)}, u32[]{:S(2)}) async-start(f32[1,8,256,256]{3,1,0,2:T(8,128)} %copy.103), calls=%async_computation.3 | async-start | bytes 4194304 | tf_op jit(solution)/shard_map/all_to_all | solution.py:101
  30.3 4.1 %copy.89 = f32[1,8,256,256]{3,1,0,2:T(8,128)} copy(f32[1,8,256,256]{3,2,1,0:T(8,128)} %get-tuple-element.284) | data formatting | bytes 4194304 | tf_op jit(solution)/shard_map/add | solution.py:84
  34.4 21.6 %all-to-all-done.3 = f32[1,8,256,256]{3,1,0,2:T(8,128)} async-done(((f32[1,8,256,256]{3,1,0,2:T(8,128)}), f32[1,8,256,256]{3,1,0,2:T(8,128)}, u32[]{:S(2)}, u32[]{:S(2)}) %all-to-all-start.3) | async-done | bytes 2097184 | tf_op jit(solution)/shard_map/all_to_all | solution.py:101
  56.0 4.4 %all-to-all-start = ((f32[1,8,256,256]{3,1,0,2:T(8,128)}), f32[1,8,256,256]{3,1,0,2:T(8,128)}, u32[]{:S(2)}, u32[]{:S(2)}) async-start(f32[1,8,256,256]{3,1,0,2:T(8,128)} %copy.89), calls=%async_computation | async-start | bytes 4194304 | tf_op jit(solution)/shard_map/all_to_all | solution.py:100
  60.5 3.6 %copy.173 = f32[1,8,4,64,256]{4,3,1,0,2:T(8,128)} copy(f32[1,8,4,64,256]{4,1,3,2,0:T(8,128)} %bitcast.39) | data formatting | bytes 4194304 | tf_op jit(solution)/shard_map/all_to_all | solution.py:101
  64.1 22.1 %all-to-all-done = f32[1,8,256,256]{3,1,0,2:T(8,128)} async-done(((f32[1,8,256,256]{3,1,0,2:T(8,128)}), f32[1,8,256,256]{3,1,0,2:T(8,128)}, u32[]{:S(2)}, u32[]{:S(2)}) %all-to-all-start) | async-done | bytes 2097184 | tf_op jit(solution)/shard_map/all_to_all | solution.py:100
  86.2 2.4 copy.90
  91.1 21.7 %all-gather.1 = f32[8,1,8]{2,1,0:T(1,128)S(1)} all-gather(f32[1,1,8]{2,1,0:T(1,128)S(1)} %get-tuple-element.269), channel_id=1, replica_groups=mesh['grp'=8,'mem'=4] {'grp'}, dimensions={0}, use_global_device_ids=true | all-gather | bytes 288 | tf_op jit(solution)/shard_map/all_gather | solution.py:14
  112.8 16.6 %all-gather = f32[8,1,8]{2,1,0:T(1,128)S(1)} all-gather(f32[1,1,8]{2,1,0:T(1,128)S(1)} %get-tuple-element.270), channel_id=1, replica_groups=mesh['grp'=8,'mem'=4] {'grp'}, dimensions={0}, use_global_device_ids=true | all-gather | bytes 288 | tf_op jit(solution)/shard_map/all_gather | solution.py:14
  129.4 34.7 %all-gather.7.cloned.1.call-done = f32[8,8,64,256]{3,2,1,0:T(8,128)} async-done(((f32[1,8,64,256]{3,2,1,0:T(8,128)}), f32[8,8,64,256]{3,2,1,0:T(8,128)}) %all-gather.7.cloned.1.call-update) | async-done | bytes 4194320 | tf_op jit(solution)/shard_map/all_gather | solution.py:14
  164.1 4.7 %rev.6 = f32[8,8,64,256]{3,2,1,0:T(8,128)} reverse(f32[8,8,64,256]{3,2,1,0:T(8,128)} %all-gather.7.cloned.1.call-done), dimensions={0} | reverse | bytes 8388608 | tf_op jit(solution)/shard_map/rev | solution.py:16
  168.8 8.5 %while.29 = (s32[]{:T(128)}, f32[8,64,256]{2,1,0:T(8,128)S(1)}, s32[]{:T(128)}, f32[8,8,64,256]{3,2,1,0:T(8,128)}, f32[8,8]{1,0:T(8,128)S(1)}, /*index=5*/s32[]{:T(128)}, s32[]{:T(128)}) while((s32[]{:T(128)}, f32[8,64,256]{2,1,0:T(8,128)S(1)}, s32[]{:T(128)}, f32[8,8,64,256]{3,2,1,0:T(8,128)}, f32[8,8]{1,0:T(8,128)S(1)}, ...), condition=%wide.region_4.5_spmd.clone, body=%wide.region_3.4_spmd.clone.sunk | while | flops 524292 | bytes 1573073 | solution.py:26
  180.6 4.4 %all-to-all-start.4 = ((f32[4,8,64,256]{3,2,1,0:T(8,128)}), f32[4,8,64,256]{3,2,1,0:T(8,128)}, u32[]{:S(2)}, u32[]{:S(2)}) async-start(f32[4,8,64,256]{3,2,1,0:T(8,128)} %pad_maximum_fusion.1), calls=%async_computation.4 | async-start | bytes 4194304 | tf_op jit(solution)/shard_map/all_to_all | solution.py:130
  185.1 52.5 %all-gather.5.cloned.1.call-done = f32[8,8,64,256]{3,2,1,0:T(8,128)} async-done(((f32[1,8,64,256]{3,2,1,0:T(8,128)}), f32[8,8,64,256]{3,2,1,0:T(8,128)}) %all-gather.5.cloned.1.call-update) | async-done | bytes 4194320 | tf_op jit(solution)/shard_map/all_gather | solution.py:14
  237.6 8.5 %while.28 = (s32[]{:T(128)}, f32[8,64,256]{2,1,0:T(8,128)S(1)}, s32[]{:T(128)}, f32[8,8,64,256]{3,2,1,0:T(8,128)}, f32[8,8]{1,0:T(8,128)S(1)}, /*index=5*/s32[]{:T(128)}, s32[]{:T(128)}) while((s32[]{:T(128)}, f32[8,64,256]{2,1,0:T(8,128)S(1)}, s32[]{:T(128)}, f32[8,8,64,256]{3,2,1,0:T(8,128)}, f32[8,8]{1,0:T(8,128)S(1)}, ...), condition=%wide.region_2.3_spmd.clone, body=%wide.region_1.2_spmd.clone.sunk | while | flops 524292 | bytes 1573073 | solution.py:26
  249.3 4.8 %all-to-all-start.2 = ((f32[4,8,64,256]{3,2,1,0:T(8,128)}), f32[4,8,64,256]{3,2,1,0:T(8,128)}, u32[]{:S(2)}, u32[]{:S(2)}) async-start(f32[4,8,64,256]{3,2,1,0:T(8,128)} %pad_maximum_fusion), calls=%async_computation.2 | async-start | bytes 4194304 | tf_op jit(solution)/shard_map/all_to_all | solution.py:129
  254.1 2.7 fusion.14
  258.7 2.3 fusion.24
  261.0 2.1 fusion.28
  263.1 16.5 %all-to-all-done.2 = f32[4,8,64,256]{3,2,1,0:T(8,128)} async-done(((f32[4,8,64,256]{3,2,1,0:T(8,128)}), f32[4,8,64,256]{3,2,1,0:T(8,128)}, u32[]{:S(2)}, u32[]{:S(2)}) %all-to-all-start.2) | async-done | bytes 2097184 | tf_op jit(solution)/shard_map/all_to_all | solution.py:129
  287.9 3.2 %fusion.5 = bf16[2,128,8,256]{3,1,2,0:T(8,128)(2,1)} fusion(f32[2,8,256,128]{2,3,1,0:T(8,128)} %fusion.28, f32[2,128,8]{1,2,0:T(8,128)S(1)} %get-tuple-element.264, bf16[2,128,8,256]{3,2,1,0:T(8,128)(2,1)S(1)} %bitcast.295, bf16[2,128,8,256]{3,2,1,0:T(8,128)(2,1)S(1)} %bitcast.288, bf16[2,128,8,256]{3,2,1,0:T(8,128)(2,1)S(1)} %bitcast.299, ...), kind=kOutput, calls=%fused_computation.18 | convolution fusion | flops 271843328 | bytes 6324224 | tf_op jit(solution)/shard_map/bhts,bthe->bshe/dot_general | solution.py:63
  (106 shorter events, 47.5 us)
Async XLA Ops:
  7.2 8.1 %copy-start.14 = (bf16[256,2048]{1,0:T(8,128)(2,1)S(1)}, bf16[256,2048]{1,0:T(8,128)(2,1)}, u32[]{:S(2)}) copy-start(bf16[256,2048]{1,0:T(8,128)(2,1)} %param.12) | copy-start | bytes 3145732
  9.3 16.5 %all-to-all-start.1 = ((f32[1,8,4,1]{1,3,0,2:T(1,128)}), f32[1,8,4,1]{1,3,0,2:T(1,128)S(1)}, u32[]{:S(2)}, u32[]{:S(2)}) async-start(f32[1,8,4,1]{1,3,0,2:T(1,128)} %broadcast_in_dim.21), calls=%async_computation.1 | async-start | bytes 4096 | tf_op jit(solution)/shard_map/all_to_all | solution.py:99
  13.6 2.0 copy-start.15
  15.2 2.4 copy-start.4
  15.2 2.0 copy-start.16
  15.6 2.0 copy-start.6
  15.9 3.1 %copy-start.9 = (bf16[32,8,8,256]{3,2,1,0:T(8,128)(2,1)}, bf16[32,8,8,256]{3,2,1,0:T(8,128)(2,1)S(1)}, u32[]{:S(2)}) copy-start(bf16[32,8,8,256]{3,2,1,0:T(8,128)(2,1)S(1)} %copy.132) | copy-start | bytes 3145732
  17.6 1.4 copy-start
  25.8 30.2 %all-to-all-start.3 = ((f32[1,8,256,256]{3,1,0,2:T(8,128)}), f32[1,8,256,256]{3,1,0,2:T(8,128)}, u32[]{:S(2)}, u32[]{:S(2)}) async-start(f32[1,8,256,256]{3,1,0,2:T(8,128)} %copy.103), calls=%async_computation.3 | async-start | bytes 4194304 | tf_op jit(solution)/shard_map/all_to_all | solution.py:101
  56.0 30.2 %all-to-all-start = ((f32[1,8,256,256]{3,1,0,2:T(8,128)}), f32[1,8,256,256]{3,1,0,2:T(8,128)}, u32[]{:S(2)}, u32[]{:S(2)}) async-start(f32[1,8,256,256]{3,1,0,2:T(8,128)} %copy.89), calls=%async_computation | async-start | bytes 4194304 | tf_op jit(solution)/shard_map/all_to_all | solution.py:100
  60.4 103.7 %all-gather.7.cloned.1.call-start = ((), (), s32[]{:S(2)}) async-start(), calls=%async_computation.6 | async-start | bytes 4718592 | tf_op jit(solution)/shard_map/all_gather | solution.py:14
  86.2 2.4 copy-start.3
  88.6 1.7 copy-start.2
  90.3 147.3 %all-gather.5.cloned.1.call-start = ((), (), s32[]{:S(2)}) async-start(), calls=%async_computation.5 | async-start | bytes 4718592 | tf_op jit(solution)/shard_map/all_gather | solution.py:14
  180.6 68.7 %all-to-all-start.4 = ((f32[4,8,64,256]{3,2,1,0:T(8,128)}), f32[4,8,64,256]{3,2,1,0:T(8,128)}, u32[]{:S(2)}, u32[]{:S(2)}) async-start(f32[4,8,64,256]{3,2,1,0:T(8,128)} %pad_maximum_fusion.1), calls=%async_computation.4 | async-start | bytes 4194304 | tf_op jit(solution)/shard_map/all_to_all | solution.py:130
  249.3 4.8 %copy-start.7 = (bf16[32,8,8,256]{3,2,1,0:T(8,128)(2,1)S(1)}, bf16[32,8,8,256]{3,2,1,0:T(8,128)(2,1)}, u32[]{:S(2)}) copy-start(bf16[32,8,8,256]{3,2,1,0:T(8,128)(2,1)} %copy-done.6) | copy-start | bytes 3145732
  249.3 30.3 %all-to-all-start.2 = ((f32[4,8,64,256]{3,2,1,0:T(8,128)}), f32[4,8,64,256]{3,2,1,0:T(8,128)}, u32[]{:S(2)}, u32[]{:S(2)}) async-start(f32[4,8,64,256]{3,2,1,0:T(8,128)} %pad_maximum_fusion), calls=%async_computation.2 | async-start | bytes 4194304 | tf_op jit(solution)/shard_map/all_to_all | solution.py:129
  256.8 1.9 copy-start.10
  258.7 2.3 copy-start.1
  263.1 18.4 %copy-start.8 = (bf16[32,8,8,256]{3,2,1,0:T(8,128)(2,1)S(1)}, bf16[32,8,8,256]{3,2,1,0:T(8,128)(2,1)}, u32[]{:S(2)}) copy-start(bf16[32,8,8,256]{3,2,1,0:T(8,128)(2,1)} %copy-done.6) | copy-start | bytes 3145732
  279.6 2.2 copy-start.11
  281.8 1.0 copy-start.13
  283.4 1.9 copy-start.5
  283.4 1.9 copy-start.12
Sparse Core Ops, SparseCore 0:
  90.4 73.6 all-gather.6
  166.2 71.3 all-gather.4
where the time goes:
time: 303 us; the launch traced here: 301 us
  waiting for transfers between devices  148 us (49%)
  blocking collectives  38.3 us (13%)
  local copies, waits for them, and re-layouts  33.3 us (11%)
  other arithmetic  28.9 us (10%)
  starting transfers between devices  22.4 us (7%)
  matrix products  15 us (5%)
  between operations  14.4 us (5%)
    all_gather x2, waiting for transfers between devices, prefix(): pieces = jax.tree.map(lambda part: lax.all_gather(part, axis), value)  87.2 us
    all_gather x2, blocking collectives, prefix(): pieces = jax.tree.map(lambda part: lax.all_gather(part, axis), value)  38.3 us
    all_to_all x1, waiting for transfers between devices, body(): lax.all_to_all(forward_total[None], 'mem', split_axis=2, concat_axis=0, t...  22.1 us
    all_to_all x1, waiting for transfers between devices, body(): lax.all_to_all(running[None], 'mem', split_axis=2, concat_axis=0, tiled=T...  21.6 us
    all_to_all x1, waiting for transfers between devices, body(): lax.all_to_all(first_stack, 'mem', split_axis=0, concat_axis=2, tiled=True)  16.5 us
    select_n x14, other arithmetic, turn(): jnp.where(position < mine, new, old)  16.5 us
    unnamed x41, local copies, waits for them, and re-layouts  8.32 us
  transfers between devices with their start and end apart: 7, of which 5 were waited for; matrix products, arithmetic and copies ran while one was open for 18% of the time, Pallas kernels for 0%

commit v1 on v0

v1 whole, which is shorter than its diff:
```python
import functools

import jax
import jax.numpy as jnp
from jax import lax
from jax.experimental import pallas as pl
from jax.experimental.pallas import tpu as pltpu
from jax.sharding import PartitionSpec as P

HEAD_COUNT = 8
DK = 256
DV = 256
BLOCK = 128
CORES = 2
MESH = pl.DeviceIdType.MESH
F32 = jnp.float32
BF16 = jnp.bfloat16


def dot(a, b, ca, cb):
    return lax.dot_general(a, b, (((ca,), (cb,)), ((), ())), preferred_element_type=F32)


def block_cumul(logs_ref, head, b):
    tile = logs_ref[:, b * BLOCK:(b + 1) * BLOCK]
    pick = lax.broadcasted_iota(jnp.int32, tile.shape, 0) == head
    row = jnp.broadcast_to(
        jnp.sum(jnp.where(pick, tile, 0.0), axis=0, keepdims=True), (8, BLOCK)
    )
    lane = lax.broadcasted_iota(jnp.int32, (8, BLOCK), 1)
    step = 1
    while step < BLOCK:
        row = row + jnp.where(lane >= step, pltpu.roll(row, step, 1), 0.0)
        step *= 2
    return row[0:1, :]


def spread_rows(row):
    flat = jnp.broadcast_to(row, (BLOCK, BLOCK))
    return flat, flat.T


def wide(mat, width):
    return jnp.concatenate([mat] * (width // BLOCK), axis=1)


def totals_kernel(count, logs_ref, q_ref, k_ref, v_ref, g_ref, f_ref, r_ref, d_ref):
    head = pl.program_id(0)
    forward = None
    carried = None
    reverse = []
    for b in range(count):
        rows = slice(b * BLOCK, (b + 1) * BLOCK)
        row = block_cumul(logs_ref, head, b)
        _, cols = spread_rows(row)
        end = row[:, BLOCK - 1:BLOCK]
        tail = wide(jnp.exp(end - cols), DK)
        front = wide(jnp.exp(cols), DK)
        kd = (k_ref[rows, :].astype(F32) * tail).astype(BF16)
        qd = (q_ref[rows, :].astype(F32) * front).astype(BF16)
        part = dot(kd, v_ref[rows, :], 0, 0)
        whole = jnp.broadcast_to(jnp.exp(end), (1, DV))
        forward = part if forward is None else whole * forward + part
        carried = whole if carried is None else carried * whole
        reverse.append((whole, dot(qd, g_ref[rows, :], 0, 0)))
    back = None
    for whole, part in reversed(reverse):
        back = part if back is None else whole * back + part
    f_ref[0] = forward
    r_ref[0] = back
    d_ref[0] = carried


def final_kernel(count, logs_ref, q_ref, k_ref, v_ref, g_ref, s_ref, e_ref, gq_ref, gk_ref, gv_ref):
    head = pl.program_id(0)
    scale = DK ** (-0.5)
    lower = lax.broadcasted_iota(jnp.int32, (BLOCK, BLOCK), 0) >= lax.broadcasted_iota(
        jnp.int32, (BLOCK, BLOCK), 1
    )
    state = s_ref[0]
    saved = []
    for b in range(count):
        rows = slice(b * BLOCK, (b + 1) * BLOCK)
        row = block_cumul(logs_ref, head, b)
        flat, cols = spread_rows(row)
        end = row[:, BLOCK - 1:BLOCK]
        decay = jnp.where(lower, jnp.exp(jnp.where(lower, cols - flat, 0.0)), 0.0)
        tail = wide(jnp.exp(end - cols), DK)
        front = wide(jnp.exp(cols), DK)
        whole = jnp.broadcast_to(jnp.exp(end), (1, DV))
        q, k, v, g = q_ref[rows, :], k_ref[rows, :], v_ref[rows, :], g_ref[rows, :]
        wg = (dot(g, v, 1, 1) * decay).astype(BF16)
        wv = (dot(q, k, 1, 1) * decay).astype(BF16)
        low = state.astype(BF16)
        gq_ref[rows, :] = (scale * (dot(wg, k, 1, 0) + front * dot(g, low, 1, 1))).astype(BF16)
        if b < count - 1:
            kd = (k.astype(F32) * tail).astype(BF16)
            state = whole * state + dot(kd, v, 0, 0)
        saved.append((rows, tail, front, whole, wg, wv))
    grads = e_ref[0]
    for b in reversed(range(count)):
        rows, tail, front, whole, wg, wv = saved[b]
        q, k, v, g = q_ref[rows, :], k_ref[rows, :], v_ref[rows, :], g_ref[rows, :]
        low = grads.astype(BF16)
        gk_ref[rows, :] = (scale * (dot(wg, q, 0, 0) + tail * dot(v, low, 1, 1))).astype(BF16)
        gv_ref[rows, :] = (scale * (dot(wv, g, 0, 0) + tail * dot(k, low, 1, 0))).astype(BF16)
        if b > 0:
            qd = (q.astype(F32) * front).astype(BF16)
            grads = whole * grads + dot(qd, g, 0, 0)


def scan_kernel(
    nx, ny, nz, f_ref, r_ref, d_ref, fo_ref, ro_ref,
    peer_buf, chip_buf, plane_buf, out_buf, ztot, zbuf, acc, ret_buf, back_buf,
    dpeer, dchip, dplane, dtot, dz,
    s_core, r_core, s_plane, r_plane, s_z, r_z, s_ret, r_ret, s_back, r_back,
    s_dc, r_dc, s_dp, r_dp, s_dz, r_dz,
):
    chips = nx * ny
    half = HEAD_COUNT // CORES
    width = DK // chips
    group = max(1, half // 2)
    chunks = [(d, k) for k in range(half // group) for d in range(2)]
    number = {c: n for n, c in enumerate(chunks)}
    grp, mem = lax.axis_index("grp"), lax.axis_index("mem")
    z, y = grp // ny, lax.rem(grp, ny)
    x, core = mem // CORES, lax.rem(mem, CORES)
    chip = y * nx + x
    mate = (grp, x * CORES + 1 - core)

    def chip_id(c):
        return (z * ny + c // nx, lax.rem(c, nx) * CORES + core)

    def z_id(to):
        return (to * ny + y, mem)

    others = [lax.rem(chip + off, chips) for off in range(1, chips)]
    zs = [lax.rem(z + off, nz) for off in range(1, nz)]
    peers = [mate] + [chip_id(c) for c in others] + [z_id(t) for t in zs]
    barrier = pltpu.get_barrier_semaphore()
    for peer in peers:
        pl.semaphore_signal(barrier, inc=1, device_id=peer, device_id_type=MESH)
    pl.semaphore_wait(barrier, len(peers))

    def copy(src, dst, send, recv, device):
        return pltpu.make_async_remote_copy(
            src_ref=src, dst_ref=dst, send_sem=send, recv_sem=recv,
            device_id=device, device_id_type=MESH,
        )

    sent = []

    def go(*args):
        c = copy(*args)
        c.start()
        sent.append(c)

    ins = (f_ref, r_ref)
    outs = (fo_ref, ro_ref)
    mine, theirs = core * half, (1 - core) * half

    def span(k):
        return pl.ds(k * group, group)

    def block(c):
        return pl.ds(pl.multiple_of(c * width, width), width)

    go(d_ref, dpeer, s_dc, r_dc, mate)
    for n, (d, k) in enumerate(chunks):
        go(ins[d].at[pl.ds(theirs + k * group, group)], peer_buf.at[d, span(k)],
           s_core.at[n], r_core.at[n], mate)
    copy(d_ref, dpeer, s_dc, r_dc, mate).wait_recv()
    dchip[...] = d_ref[...] * dpeer[...]
    dplane[chip] = d_ref[...] * dpeer[...]
    for o in others:
        go(dchip, dplane.at[chip], s_dp.at[o], r_dp.at[chip], chip_id(o))
    first = core == 0
    for n, (d, k) in enumerate(chunks):
        copy(peer_buf.at[d, span(k)], peer_buf.at[d, span(k)],
             s_core.at[n], r_core.at[n], mate).wait_recv()
        for j in range(k * group, (k + 1) * group):
            own_d = d_ref[mine + j]
            peer_d = dpeer[mine + j]
            one = jnp.ones_like(own_d)
            if d == 0:
                w_own, w_peer = jnp.where(first, peer_d, one), jnp.where(first, one, own_d)
            else:
                w_own, w_peer = jnp.where(first, one, peer_d), jnp.where(first, own_d, one)
            chip_buf[d, j] = w_own * ins[d][mine + j] + w_peer * peer_buf[d, j]
            plane_buf[chip, d, j] = chip_buf[d, j, block(chip), :]
        for o in others:
            go(chip_buf.at[d, span(k), block(o), :], plane_buf.at[chip, d, span(k)],
               s_plane.at[o, n], r_plane.at[chip, n], chip_id(o))

    for o in others:
        copy(dchip, dplane.at[o], s_dp.at[o], r_dp.at[o], chip_id(o)).wait_recv()
    total = dplane[0]
    for c in range(1, chips):
        total = total * dplane[c]
    dtot[...] = total
    for t in zs:
        go(dtot, dz.at[z], s_dz.at[t], r_dz.at[z], z_id(t))

    zsent = []
    for n, (d, k) in enumerate(chunks):
        for o in others:
            copy(plane_buf.at[o, d, span(k)], plane_buf.at[o, d, span(k)],
                 s_plane.at[o, n], r_plane.at[o, n], chip_id(o)).wait_recv()
        order = range(chips) if d == 0 else range(chips - 1, -1, -1)
        for j in range(k * group, (k + 1) * group):
            running = jnp.zeros((width, DV), F32)
            for c in order:
                out_buf[c, d, j] = running
                running = dplane[c, mine + j] * running + plane_buf[c, d, j]
            ztot[d, j] = running
        for t in zs:
            c = copy(ztot.at[d, span(k)], zbuf.at[z, d, span(k)],
                     s_z.at[t, n], r_z.at[z, n], z_id(t))
            needs = (t > z) if d == 0 else (t < z)
            pl.when(needs)(c.start)
            zsent.append((needs, c))

    for t in zs:
        copy(dtot, dz.at[t], s_dz.at[t], r_dz.at[t], z_id(t)).wait_recv()
    for n, (d, k) in enumerate(chunks):
        acc[span(k)] = jnp.zeros((group, width, DV), F32)
        for t in range(nz) if d == 0 else range(nz - 1, -1, -1):
            @pl.when((t < z) if d == 0 else (t > z))
            def _():
                copy(zbuf.at[t, d, span(k)], zbuf.at[t, d, span(k)],
                     s_z.at[t, n], r_z.at[t, n], z_id(t)).wait_recv()
                for j in range(k * group, (k + 1) * group):
                    acc[j] = dz[t, mine + j] * acc[j] + zbuf[t, d, j]
        order = range(chips) if d == 0 else range(chips - 1, -1, -1)
        for j in range(k * group, (k + 1) * group):
            held = acc[j]
            weight = jnp.ones((1, DV), F32)
            for c in order:
                out_buf[c, d, j] = out_buf[c, d, j] + weight * held
                weight = weight * dplane[c, mine + j]
            ret_buf[d, j, block(chip), :] = out_buf[chip, d, j]
        for o in others:
            go(out_buf.at[o, d, span(k)], ret_buf.at[d, span(k), block(chip), :],
               s_ret.at[o, n], r_ret.at[chip, n], chip_id(o))

    for n, (d, k) in enumerate(chunks):
        for o in others:
            copy(out_buf.at[o, d, span(k)], ret_buf.at[d, span(k), block(o), :],
                 s_ret.at[o, n], r_ret.at[o, n], chip_id(o)).wait_recv()
        near = first if d == 0 else jnp.logical_not(first)
        for j in range(k * group, (k + 1) * group):
            @pl.when(near)
            def _():
                got = ret_buf[d, j]
                outs[d][mine + j] = got
                back_buf[d, j] = d_ref[mine + j] * got + ins[d][mine + j]

            @pl.when(jnp.logical_not(near))
            def _():
                got = ret_buf[d, j]
                back_buf[d, j] = got
                outs[d][mine + j] = dpeer[mine + j] * got + peer_buf[d, j]
        go(back_buf.at[d, span(k)], outs[d].at[pl.ds(mine + k * group, group)],
           s_back.at[n], r_back.at[n], mate)
    for n, (d, k) in enumerate(chunks):
        copy(back_buf.at[d, span(k)], outs[d].at[pl.ds(theirs + k * group, group)],
             s_back.at[n], r_back.at[n], mate).wait_recv()
    for c in sent:
        c.wait_send()
    for needs, c in zsent:
        pl.when(needs)(c.wait_send)


def body(nx, ny, nz, queries, keys, values, grad_out, log_decay):
    tokens = queries.shape[0]
    count = tokens // BLOCK
    chips = nx * ny
    half = HEAD_COUNT // CORES
    width = DK // chips
    state = jax.ShapeDtypeStruct((HEAD_COUNT, DK, DV), F32)
    col = pl.BlockSpec((tokens, DK), lambda h: (0, h))
    logs = pl.BlockSpec((HEAD_COUNT, tokens), lambda h: (0, 0))
    mat = pl.BlockSpec((1, DK, DV), lambda h: (h, 0, 0))
    forward, reverse, decays = pl.pallas_call(
        functools.partial(totals_kernel, count),
        grid=(HEAD_COUNT,),
        out_shape=(state, state, jax.ShapeDtypeStruct((HEAD_COUNT, 1, DV), F32)),
        in_specs=[logs, col, col, col, col],
        out_specs=(mat, mat, pl.BlockSpec((1, 1, DV), lambda h: (h, 0, 0))),
        name="totals",
    )(log_decay, queries, keys, values, grad_out)

    vm = pl.BlockSpec(memory_space=pltpu.VMEM)
    dma = pltpu.SemaphoreType.DMA
    group = max(1, half // 2)
    n = 2 * (half // group)
    both = pltpu.VMEM((2, half, DK, DV), F32)
    rows = pltpu.VMEM((HEAD_COUNT, 1, DV), F32)
    state_from, grads_from = pl.pallas_call(
        functools.partial(scan_kernel, nx, ny, nz),
        out_shape=(state, state),
        in_specs=[vm, vm, vm],
        out_specs=(vm, vm),
        scratch_shapes=[
            both, both,
            pltpu.VMEM((chips, 2, half, width, DV), F32),
            pltpu.VMEM((chips, 2, half, width, DV), F32),
            pltpu.VMEM((2, half, width, DV), F32),
            pltpu.VMEM((nz, 2, half, width, DV), F32),
            pltpu.VMEM((half, width, DV), F32),
            both, both,
            rows, rows,
            pltpu.VMEM((chips, HEAD_COUNT, 1, DV), F32),
            rows,
            pltpu.VMEM((nz, HEAD_COUNT, 1, DV), F32),
            dma((n,)), dma((n,)),
            dma((chips, n)), dma((chips, n)),
            dma((nz, n)), dma((nz, n)),
            dma((chips, n)), dma((chips, n)),
            dma((n,)), dma((n,)),
            dma, dma,
            dma((chips,)), dma((chips,)),
            dma((nz,)), dma((nz,)),
        ],
        compiler_params=pltpu.CompilerParams(collective_id=0, has_side_effects=True),
        name="scan",
    )(forward, reverse, decays)

    out = jax.ShapeDtypeStruct((tokens, HEAD_COUNT * DK), BF16)
    return pl.pallas_call(
        functools.partial(final_kernel, count),
        grid=(HEAD_COUNT,),
        out_shape=(out, out, out),
        in_specs=[logs, col, col, col, col, mat, mat],
        out_specs=(col, col, col),
        name="final",
    )(log_decay, queries, keys, values, grad_out, state_from, grads_from)


def solution(mesh):
    nx = mesh.shape["mem"] // CORES
    ny = nx if mesh.shape["grp"] % nx == 0 else 1
    nz = mesh.shape["grp"] // ny
    tokens = P(("grp", "mem"), None)
    return jax.shard_map(
        functools.partial(body, nx, ny, nz),
        mesh=mesh,
        in_specs=(tokens, tokens, tokens, tokens, P(None, ("grp", "mem"))),
        out_specs=(tokens, tokens, tokens),
        check_vma=False,
    )
```

time: 303 us -> 89 us (0.29)
  waiting for transfers between devices: 148 us -> 0 us
  Pallas kernels: 0 us -> 88 us
  blocking collectives: 38.3 us -> 0 us
  local copies, waits for them, and re-layouts: 33.3 us -> 0 us
  other arithmetic: 28.9 us -> 0 us
  starting transfers between devices: 22.4 us -> 0 us
  matrix products: 15 us -> 0 us
  between operations: 14.4 us -> 0.64 us
    pallas_call x0 -> x3, Pallas kernels: none -> 88 us  [the longest x1 63.7 us: body(): pl.pallas_call(functools.partial(scan_kernel, nx, ny, nz), out_shape=(sta...]
    all_gather x2 -> x0, waiting for transfers between devices: 87.2 us -> none  [prefix(): pieces = jax.tree.map(lambda part: lax.all_gather(part, axis), value)]
    all_to_all x5 -> x0, waiting for transfers between devices: 60.2 us -> none  [the longest x1 22.1 us: body(): lax.all_to_all(forward_total[None], 'mem', split_axis=2, concat_axis=0, t...]
    all_gather x2 -> x0, blocking collectives: 38.3 us -> none  [prefix(): pieces = jax.tree.map(lambda part: lax.all_gather(part, axis), value)]
    all_to_all x5 -> x0, starting transfers between devices: 22.3 us -> none  [the longest x1 4.76 us: body(): lax.all_to_all(first_stack, 'mem', split_axis=0, concat_axis=2, tiled=True)]
    select_n x14 -> x0, other arithmetic: 16.5 us -> none  [turn(): jnp.where(position < mine, new, old)]
    dot_general x9 -> x0, matrix products: 15 us -> none  [the longest x1 3.18 us: body(): jnp.einsum('bhts,bthe->bshe', weight_value, grad_blocks, preferred_elemen...]
    all_to_all x4 -> x0, local copies, waits for them, and re-layouts: 9.7 us -> none  [the longest x1 3.6 us: body(): lax.all_to_all(running[None], 'mem', split_axis=2, concat_axis=0, tiled=T...]
  transfers between devices with their start and end apart: 7 -> 0, of which waited for: 5 -> 0; matrix products, arithmetic and copies ran while one was open for 18% -> 0% of each run, Pallas kernels for 0% -> 0%
where the time goes in v1:
time: 89 us; the launch traced here: 88.7 us
  Pallas kernels  88 us (99%)
    pallas_call x1, Pallas kernels, body(): pl.pallas_call(functools.partial(scan_kernel, nx, ny, nz), out_shape=(sta...  63.7 us
    pallas_call x1, Pallas kernels, body(): pl.pallas_call(functools.partial(final_kernel, count), grid=(HEAD_COUNT,)...  13.3 us
    pallas_call x1, Pallas kernels, body(): pl.pallas_call(functools.partial(totals_kernel, count), grid=(HEAD_COUNT,...  10.9 us

profile of v1, /device:TPU:0, one launch (start us, length us, event | category | flops | bytes accessed | tf_op | source)
XLA Modules:
  0.0 88.7 jit_solution(13297811862465310728)
XLA Ops:
  0.6 10.9 %totals.1 = (f32[8,256,256]{2,1,0:T(8,128)}, f32[8,256,256]{2,1,0:T(8,128)}, f32[8,1,256]{2,1,0:T(1,128)}) custom-call(f32[8,256]{1,0:T(8,128)} %logs_ref.3, bf16[256,2048]{1,0:T(8,128)(2,1)} %q_ref.3, bf16[256,2048]{1,0:T(8,128)(2,1)} %k_ref.3, bf16[256,2048]{1,0:T(8,128)(2,1)} %v_ref.3, bf16[256,2048]{1,0:T(8,128)(2,1)} %g_ref.3), custom_call_target="tpu_custom_call" | custom-call | tf_op jit(solution)/shard_map/totals/pallas_call | solution.py:284
  11.6 63.7 %scan.1 = (f32[8,256,256]{2,1,0:T(8,128)}, f32[8,256,256]{2,1,0:T(8,128)}) custom-call(f32[8,256,256]{2,1,0:T(8,128)} %get-tuple-element.8.f_ref, f32[8,256,256]{2,1,0:T(8,128)} %get-tuple-element.9.r_ref, f32[8,1,256]{2,1,0:T(1,128)} %get-tuple-element.10.d_ref), custom_call_target="tpu_custom_call" | custom-call | tf_op jit(solution)/shard_map/scan/pallas_call | solution.py:299
  75.3 13.3 %final.1 = (bf16[256,2048]{1,0:T(8,128)(2,1)}, bf16[256,2048]{1,0:T(8,128)(2,1)}, bf16[256,2048]{1,0:T(8,128)(2,1)}) custom-call(f32[8,256]{1,0:T(8,128)} %logs_ref.3, bf16[256,2048]{1,0:T(8,128)(2,1)} %q_ref.3, bf16[256,2048]{1,0:T(8,128)(2,1)} %k_ref.3, bf16[256,2048]{1,0:T(8,128)(2,1)} %v_ref.3, bf16[256,2048]{1,0:T(8,128)(2,1)} %g_ref.3, ...), custom_call_target="tpu_custom_call" | custom-call | tf_op jit(solution)/shard_map/final/pallas_call | solution.py:330
